TPU v7x, 256 devices: a 4x2x16 block of a 4x16x16 slice. The times are simulated.
256 devices in a mesh: win: 2 (over y), row: 128 (over x, z, core).
Axes of the slice: x: 4, y: 2, z: 16, core: 2. Of those that a mesh axis runs over, the one named last changes fastest.
The devices are a block of a 4x16x16 slice.
Arguments:
- spectra: bfloat16 [256, 2, 32768], P(('win', 'row')), parts along dimension 0, may hold values from -6 to 6
- pair_mask: int32 [128, 128], P('row'), may hold values from 0 to 1, as said below
- available: int32 [256], P('win'), parts along dimension 0, may hold values 0 or 1
Outputs:
- correlations: float32 [256, 128, 8192], P(('win', 'row')), parts along dimension 0
There are 2 independent parts, one for each index of `win`. A program takes and returns all parts, laid end to end along the dimension named above; an argument that names none is the same for every part. Nothing has to cross between parts.
Inputs may be any that keep to these rules, and one draw needn't show every extreme that they name: pair_mask[i, j] is 0 wherever j <= i.
All inputs are finite; a program needn't handle non-finite values.
Results may differ from a plain program's by a relative error of at most 0.0003.
Values may be sent and summed in bfloat16 or wider, within the bound.
No kernel may reach another device: no remote copies, remote signals or barrier semaphores. Data moves between devices by JAX's collectives and lax.ppermute only.
A program may use at most 128 MiB of HBM per device.

v0:
```python
import math

import jax
import jax.numpy as jnp
from jax import lax
from jax.sharding import PartitionSpec as P

LAGS = 8192


full_turn = 2.0 * math.pi


def build_tables(freq, lags):
    nfft = 2 * freq
    inner = min(128, lags // 2)
    column = nfft // inner
    depth = freq // column
    outer = lags // inner
    centre = lags // 2
    t_inner = jnp.arange(inner, dtype=jnp.int32)
    k_depth = jnp.arange(depth, dtype=jnp.int32)
    k_column = jnp.arange(column, dtype=jnp.int32)
    t_outer = jnp.arange(outer, dtype=jnp.int32)
    first = full_turn * (t_inner[:, None] * k_depth[None, :] % inner).astype(jnp.float32) / inner
    cos_first = jnp.cos(first)
    sin_first = jnp.sin(first)
    section_one = jnp.concatenate(
        [
            jnp.concatenate([cos_first, -sin_first], axis=1),
            jnp.concatenate([sin_first, cos_first], axis=1),
        ],
        axis=0,
    )
    twist = (
        full_turn
        * jnp.mod(k_column[None, :] * (t_inner[:, None] - centre), nfft).astype(jnp.float32)
        / nfft
    )
    second = (
        full_turn * (t_outer[:, None] * k_column[None, :] % column).astype(jnp.float32) / column
    )
    section_two = jnp.stack([jnp.cos(second), -jnp.sin(second)], axis=1)
    return (section_one, jnp.cos(twist), jnp.sin(twist), section_two)


def pair_block(own_wide, part, signs, tables):
    section_one, twist_cos, twist_sin, section_two = tables
    count = own_wide.shape[0]
    width = part.shape[0]
    freq = part.shape[2]
    inner = twist_cos.shape[0]
    column = twist_cos.shape[1]
    outer = section_two.shape[0]
    depth = freq // column
    other = part.astype(jnp.float32)
    real_part = (
        own_wide[:, None, 0, :] * other[None, :, 0, :]
        + own_wide[:, None, 1, :] * other[None, :, 1, :]
    )
    imag_part = (
        own_wide[:, None, 0, :] * other[None, :, 1, :]
        - own_wide[:, None, 1, :] * other[None, :, 0, :]
    ) * signs[:, :, None]
    cross = jnp.stack([real_part, imag_part], axis=2).reshape(count * width, 2 * depth, column)
    mixed = jnp.einsum("uv,pvk->puk", section_one, cross, precision=lax.Precision.HIGH)
    mixed = mixed.reshape(count * width, 2, inner, column)
    turned_real = mixed[:, 0] * twist_cos - mixed[:, 1] * twist_sin
    turned_imag = mixed[:, 0] * twist_sin + mixed[:, 1] * twist_cos
    turned = jnp.stack([turned_real, turned_imag], axis=1)
    summed = jnp.einsum("tck,pcuk->ptu", section_two, turned, precision=lax.Precision.HIGH)
    summed = summed.reshape(count, width, outer * inner)
    return (2.0 * summed - real_part[:, :, :1]) * (1.0 / math.sqrt(8.0 * freq))


def correlate(own, others, signs, tables):
    own_wide = own.astype(jnp.float32)
    count = own.shape[0]
    total = others.shape[0]
    width = math.gcd(total, max(1, 8 // count))
    groups = total // width
    pieces = others.reshape(groups, width, 2, others.shape[2])
    sign_pieces = jnp.transpose(signs.reshape(count, groups, width), (1, 0, 2))

    def one_group(item):
        return pair_block(own_wide, item[0], item[1], tables)

    results = lax.map(one_group, (pieces, sign_pieces))
    return jnp.transpose(results, (1, 0, 2, 3)).reshape(count, total, results.shape[3])


def per_device(spectra, pair_mask, available):
    count = spectra.shape[0]
    freq = spectra.shape[2]
    tables = build_tables(freq, LAGS)
    first_station = lax.axis_index("row") * count
    own_flags = lax.dynamic_slice_in_dim(available, first_station, count, 0).astype(jnp.float32)
    weight = (
        pair_mask.astype(jnp.float32) * own_flags[:, None] * available.astype(jnp.float32)[None, :]
    )
    piece = lax.all_gather(spectra, "row", axis=0, tiled=True)
    corr = correlate(spectra, piece, jnp.ones((count, piece.shape[0]), jnp.float32), tables)
    return corr * weight[:, :, None]


def solution(mesh):
    return jax.shard_map(
        per_device,
        mesh=mesh,
        in_specs=(P(("win", "row"), None, None), P("row", None), P("win")),
        out_specs=P(("win", "row"), None, None),
        check_vma=False,
    )
```

profile of v0, /device:TPU:33, one launch (start us, length us, event | category | flops | bytes accessed | tf_op | source)
XLA Modules:
  0.0 506.9 jit_solution(1056133077329128225)
XLA Ops:
  12.1 166.8 %all-gather.2.cloned.1.call-done = bf16[128,2,32768]{2,1,0:T(2,128)(2,1)} async-done(((bf16[1,2,32768]{2,1,0:T(2,128)(2,1)}), bf16[128,2,32768]{2,1,0:T(2,128)(2,1)}) %all-gather.2.cloned.1.call-update) | async-done | bytes 16777232 | tf_op jit(solution)/shard_map/all_gather | solution.py:101
  178.9 316.4 %while.13 = (s32[]{:T(128)}, f32[16,1,8,8192]{3,2,1,0:T(8,128)}, f32[1,2,32768]{2,1,0:T(2,128)S(1)}, bf16[16,8,2,32768]{3,2,1,0:T(2,128)(2,1)}, f32[256,128]{1,0...) while((s32[]{:T(128)}, f32[16,1,8,8192]{3,2,1,0:T(8,128)}, ...), condition=%wide.region_1.2_spmd.clone.clone.clone, body=%wide.region_0.1_spmd.clone.clone.clone.sunk | while | flops 1215889408 | bytes 57017112 | solution.py:88
  184.3 2.9 copy.24
  187.3 4.0 reshape.466
  192.9 2.2 fusion.71
  204.1 2.9 copy.24
  207.0 4.0 reshape.466
  223.9 2.9 copy.24
  226.8 4.0 reshape.466
  232.5 2.2 fusion.71
  243.7 2.9 copy.24
  246.6 4.0 reshape.466
  252.3 2.2 fusion.71
  263.4 2.9 copy.24
  266.4 4.0 reshape.466
  272.0 2.2 fusion.71
  283.2 2.9 copy.24
  286.1 4.0 reshape.466
  291.8 2.2 fusion.71
  303.0 2.9 copy.24
  305.9 4.0 reshape.466
  311.6 2.2 fusion.71
  322.8 2.9 copy.24
  325.7 4.0 reshape.466
  331.4 2.2 fusion.71
  342.5 2.9 copy.24
  345.5 4.0 reshape.466
  351.1 2.2 fusion.71
  362.3 2.9 copy.24
  365.2 4.0 reshape.466
  370.9 2.2 fusion.71
  382.1 2.9 copy.24
  385.0 4.0 reshape.466
  390.7 2.2 fusion.71
  401.9 2.9 copy.24
  404.8 4.0 reshape.466
  421.7 2.9 copy.24
  424.6 4.0 reshape.466
  430.3 2.2 fusion.71
  441.4 2.9 copy.24
  444.4 4.0 reshape.466
  450.0 2.2 fusion.71
  461.2 2.9 copy.24
  464.1 4.0 reshape.466
  469.8 2.2 fusion.71
  481.0 2.9 copy.24
  483.9 4.0 reshape.466
  495.3 4.7 bitcast_multiply_fusion.4
  (271 shorter events, 180.8 us)
Async XLA Ops:
  6.5 172.4 %all-gather.2.cloned.1.call-start = ((), (), s32[]{:S(2)}) async-start(), calls=%async_computation | async-start | bytes 16908288 | tf_op jit(solution)/shard_map/all_gather | solution.py:101
  191.3 1.6 copy-start
  211.1 1.6 copy-start
  230.8 1.6 copy-start
  250.6 1.6 copy-start
  270.4 1.6 copy-start
  290.2 1.6 copy-start
  310.0 1.6 copy-start
  329.7 1.6 copy-start
  349.5 1.6 copy-start
  369.3 1.6 copy-start
  389.1 1.6 copy-start
  408.8 1.6 copy-start
  428.6 1.6 copy-start
  448.4 1.6 copy-start
  468.2 1.6 copy-start
  488.0 1.6 copy-start
Sparse Core Ops, SparseCore 0:
  10.0 168.9 all-gather.1
where the time goes:
time: 508 us; the launch traced here: 507 us
  waiting for transfers between devices  168 us (33%)
  local copies, waits for them, and re-layouts  168 us (33%)
  other arithmetic  89.5 us (18%)
  matrix products  66.9 us (13%)
  between operations  14.1 us (3%)
    all_gather x1, waiting for transfers between devices, per_device(): piece = lax.all_gather(spectra, 'row', axis=0, tiled=True)  167 us
    reshape x16, local copies, waits for them, and re-layouts, pair_block(): jnp.stack([real_part, imag_part], axis=2)  64.5 us
    another operation x16, local copies, waits for them, and re-layouts, pair_block(): jnp.stack([real_part, imag_part], axis=2)  47 us
    dot_general x16, matrix products, pair_block(): jnp.einsum('uv,pvk->puk', section_one, cross, precision=lax.Precision.HIGH)  34.5 us
    dot_general x16, matrix products, pair_block(): jnp.einsum('tck,pcuk->ptu', section_two, turned, precision=lax.Precision....  32.4 us
    dynamic_slice x16, local copies, waits for them, and re-layouts, correlate(): results = lax.map(one_group, (pieces, sign_pieces))  31.2 us
    slice x16, other arithmetic, pair_block(): return (2.0 * summed - real_part[:, :, :1]) * (1.0 / math.sqrt(8.0 * freq))  24 us
    slice x32, local copies, waits for them, and re-layouts, pair_block(): return (2.0 * summed - real_part[:, :, :1]) * (1.0 / math.sqrt(8.0 * freq))  17.6 us
  transfers between devices with their start and end apart: 1, of which 1 were waited for; matrix products, arithmetic and copies ran while one was open for 1% of the time, Pallas kernels for 0%

commit v1 on v0

v1 whole, which is shorter than its diff:
```python
import functools
import math

import jax
import jax.numpy as jnp
import numpy as np
from jax import lax
from jax.experimental import pallas as pl
from jax.experimental.pallas import tpu as pltpu
from jax.sharding import PartitionSpec as P

LAGS = 8192
CORES = 2
ACROSS = 4
INNER = 128


def split_table(table):
    high = table.astype(jnp.bfloat16)
    low = (table - high.astype(np.float64)).astype(jnp.bfloat16)
    return high, low


@functools.cache
def build_tables(freq):
    nfft = 2 * freq
    column = nfft // INNER
    depth = freq // column
    width = column // 2
    outer = LAGS // INNER
    scale = 2.0 / math.sqrt(8.0 * freq)
    lag = np.arange(INNER)[:, None]
    angle = 2.0 * np.pi * ((lag * np.arange(depth)[None, :]) % INNER) / INNER
    after = 2.0 * np.pi * ((lag * (np.arange(depth)[None, :] + 1)) % INNER) / INNER
    section = np.block(
        [
            [np.cos(angle), -np.sin(angle), np.cos(after), -np.sin(after)],
            [np.sin(angle), np.cos(angle), -np.sin(after), -np.cos(after)],
        ]
    )
    first = np.concatenate(split_table(section), axis=0)
    twist = 2.0 * np.pi * ((lag * np.arange(width)[None, :]) % nfft) / nfft
    turn = np.stack([np.cos(twist), np.sin(twist)]).astype(np.float32)
    steps = np.arange(outer)[None, :] - outer // 2
    angle = 2.0 * np.pi * ((np.arange(width)[:, None] * steps) % column) / column
    section = np.concatenate([np.cos(angle), -np.sin(angle)], axis=0) * scale
    second = np.concatenate(split_table(section), axis=1)
    odd = 2 * np.arange(depth)[:, None] + 1
    angle = 2.0 * np.pi * ((odd * lag.T) % (2 * INNER)) / (2 * INNER)
    section = np.concatenate([np.cos(angle), -np.sin(angle)], axis=0) * scale
    middle = np.concatenate(split_table(section), axis=1)
    return first, turn, second, middle


def fold_body(whole_ref, out_ref):
    rows, column = whole_ref.shape
    width = column // 2
    half = rows // 2
    whole = whole_ref[...]
    right = whole[:, width:]
    down = lax.broadcasted_iota(jnp.int32, (width, width), 0)
    over = lax.broadcasted_iota(jnp.int32, (width, width), 1)
    mirror = jnp.where(down == lax.rem(width - over, width), 1.0, 0.0).astype(jnp.bfloat16)
    flipped = jnp.dot(right, mirror, preferred_element_type=jnp.float32).astype(jnp.bfloat16)
    out_ref[pl.ds(0, rows), :] = whole[:, :width]
    out_ref[pl.ds(rows, rows), :] = flipped
    extra = out_ref.shape[0] - 2 * rows
    over = lax.broadcasted_iota(jnp.int32, (extra, width), 1)
    pick = jnp.where(over == 0, 1.0, 0.0).astype(jnp.bfloat16)
    straight = lax.dot_general(
        pick, right, (((1,), (1,)), ((), ())), preferred_element_type=jnp.float32
    )
    crossed = jnp.concatenate([straight[:, half:], -straight[:, :half]], axis=1)
    out_ref[pl.ds(2 * rows, extra), :] = jnp.concatenate([straight, crossed], axis=1).astype(
        jnp.bfloat16
    )


def fold_call(whole):
    rows, column = whole.shape
    return pl.pallas_call(
        fold_body,
        out_shape=jax.ShapeDtypeStruct((2 * rows + 16, column // 2), jnp.bfloat16),
        in_specs=[pl.BlockSpec(memory_space=pltpu.VMEM)],
        out_specs=pl.BlockSpec(memory_space=pltpu.VMEM),
        cost_estimate=pl.CostEstimate(flops=1_000_000, bytes_accessed=300_000, transcendentals=0),
        name="fold",
    )(whole)


def split(value):
    high = value.astype(jnp.bfloat16)
    return high, (value - high.astype(jnp.float32)).astype(jnp.bfloat16)


def cross_spectrum(other, mine):
    parts = []
    quarter = mine.shape[0] // 4
    for n in (0, 2):
        ar, ai = mine[n * quarter : (n + 1) * quarter], mine[(n + 1) * quarter : (n + 2) * quarter]
        br, bi = other[n * quarter : (n + 1) * quarter], other[(n + 1) * quarter : (n + 2) * quarter]
        parts += [ar * br + ai * bi, ar * bi - ai * br]
    return jnp.concatenate(parts, axis=0)


def turned_columns(other, mine, first, turn):
    high, low = split(cross_spectrum(other, mine))
    wide = jnp.dot(first[...], high, preferred_element_type=jnp.float32)
    rest = jnp.dot(first[: 2 * INNER], low, preferred_element_type=jnp.float32)
    mixed = wide[: 2 * INNER] + wide[2 * INNER :] + rest
    sr, si = mixed[:INNER], mixed[INNER:]
    tc, ts = turn[0], turn[1]
    turned = jnp.concatenate([sr * tc - si * ts, sr * ts + si * tc], axis=1)
    return split(turned)


def lags_of(summed, middle):
    summed = summed.T
    outer = summed.shape[0] // 2
    parity = lax.broadcasted_iota(jnp.int32, (outer, INNER), 0) % 2
    return summed[:outer] + summed[outer:] + jnp.where(parity == 0, middle, -middle)


def stage_body(step, plan, along, info, own_w, pair_w, mine0, mine1, first, turn, second, middle, *rest):
    slab_count = sum(present for present, _ in plan)
    slabs, rest = rest[:slab_count], rest[-10:]
    own_hbm, pair_ref, held, wide, mids, kept, result_ref, listed, names, sems = rest
    x, z, c = info[0], info[1], info[2]
    sign = 2 * c - 1
    per = slabs[0].shape[0]
    size = wide.shape[1]
    count = jnp.int32(0)
    taken = 0
    for side, (present, rows) in enumerate(plan):
        if not present:
            continue
        held[pl.ds(side * per, per)] = slabs[taken][...]
        taken += 1
        zj = lax.rem(z + sign * (step - side) + along, along)
        for n in range(per):
            e = side * per + n
            xj = lax.rem(x + side * sign + 2 * (n % 2) + ACROSS, ACROSS)
            j = (xj * along + zj) * CORES + lax.rem(c + n // 2, CORES)
            names[e] = j
            for row in range(rows):
                listed[count] = e * 2 + row
                keep = (own_w if row == 0 else pair_w)[j] != 0.0
                count = count + keep.astype(jnp.int32)

    quarter = size // 4
    down = lax.broadcasted_iota(jnp.int32, wide.shape[1:], 0)
    over = lax.broadcasted_iota(jnp.int32, wide.shape[1:], 1)
    once = (over == 0) & ((down == 0) | (down == quarter))
    weight = jnp.where(once, 0.5, jnp.where((over == 0) & (down >= 2 * quarter), 0.0, 1.0))
    lane = lax.broadcasted_iota(jnp.int32, (2 * per, INNER), 1)
    spot = lax.broadcasted_iota(jnp.int32, (2 * per, INNER), 0)
    straight = jnp.zeros((2 * per, INNER), jnp.float32)
    crossed = jnp.zeros((2 * per, INNER), jnp.float32)
    for side, (present, rows) in enumerate(plan):
        for e in range(side * per, (side + 1) * per if present else 0):
            edge = held[e, size:].astype(jnp.float32)[: 2 * per]
            straight = jnp.where(spot == e, edge[:, :INNER], straight)
            crossed = jnp.where(spot == e, edge[:, INNER:], crossed)
    parts = []
    for row in range(2):
        mine = mine1 if row else mine0
        wide[row] = mine[:size].astype(jnp.float32) * weight
        edge = mine[size:].astype(jnp.float32)[: 2 * per]
        real = jnp.where(lane < INNER // 2, edge[:, :INNER], -edge[:, INNER:])
        imag = jnp.where(lane < INNER // 2, edge[:, INNER:], edge[:, :INNER])
        parts.append(real * straight + imag * crossed)
    high, low = split(jnp.concatenate(parts, axis=0))
    rows_of = high.shape[0]
    summed = jnp.dot(
        jnp.concatenate([high, low], axis=0), middle[...], preferred_element_type=jnp.float32
    )
    summed = summed[:rows_of] + summed[rows_of:]
    mids[...] = summed[:, :INNER] + summed[:, INNER:]

    def copy_out(e):
        return pltpu.make_async_copy(result_ref.at[e], own_hbm.at[names[e]], sems.at[e])

    def compute(code):
        other = held[code // 2, :size].astype(jnp.float32)
        return turned_columns(other, wide[code % 2], first, turn)

    def middle_of(code):
        return mids[pl.ds(lax.rem(code, 2) * 2 * per + code // 2, 1), :]

    def keep_result(code, value):
        e = code // 2

        @pl.when(code % 2 == 0)
        def _():
            result_ref[e] = value
            copy_out(e).start()

        if pair_ref is not None:
            @pl.when(code % 2 != 0)
            def _():
                pair_ref[e] = value

    def two(k, before):
        summed = jnp.dot(kept[...], second[...], preferred_element_type=jnp.float32)
        value0 = lags_of(summed[:INNER] + summed[INNER : 2 * INNER], middle_of(before[0]))
        value1 = lags_of(summed[2 * INNER : 3 * INNER] + summed[3 * INNER :], middle_of(before[1]))
        code0 = listed[jnp.minimum(2 * k, count - 1)]
        code1 = listed[jnp.minimum(2 * k + 1, count - 1)]
        kept[...] = jnp.concatenate([*compute(code0), *compute(code1)], axis=0)

        @pl.when(k > 0)
        def _():
            keep_result(before[0], value0)

        @pl.when((k > 0) & (2 * k - 1 < count))
        def _():
            keep_result(before[1], value1)

        return code0, code1

    trips = jnp.where(count > 0, (count + 1) // 2 + 1, 0)
    lax.fori_loop(0, trips, two, (jnp.int32(0), jnp.int32(0)))
    for side, (present, rows) in enumerate(plan):
        if present:
            for n in range(per):
                e = side * per + n

                @pl.when(own_w[names[e]] != 0.0)
                def _():
                    copy_out(e).wait()


def stage_call(step, plan, along, slabs, info, own_w, pair_w, mine, tables, own_buf, pair_buf, pair_at, pair_size):
    total = own_w.shape[0]
    per = slabs[0].shape[0]
    count = 2 * per
    outer = LAGS // INNER
    smem = pl.BlockSpec(memory_space=pltpu.SMEM)
    vmem = pl.BlockSpec(memory_space=pltpu.VMEM)
    hbm = pl.BlockSpec(memory_space=pl.ANY)
    args = [info, own_w, pair_w, *mine, *tables, *slabs]
    specs = [smem] * 3 + [vmem] * (2 + len(tables) + len(slabs))
    out_shape = [jax.ShapeDtypeStruct((total, outer, INNER), jnp.float32)]
    out_specs = [hbm]
    aliases = {}
    if own_buf is not None:
        aliases[len(args)] = 0
        args.append(own_buf)
        specs.append(hbm)
    with_pair = pair_size is not None
    if with_pair:
        out_shape.append(jax.ShapeDtypeStruct((pair_size, outer, INNER), jnp.float32))
        out_specs.append(pl.BlockSpec((count, outer, INNER), lambda g: (pair_at, 0, 0)))
        if pair_buf is not None:
            aliases[len(args)] = 1
            args.append(pair_buf)
            specs.append(hbm)

    def body(*refs):
        scratch = refs[-8:]
        outs = refs[len(args) : -8]
        pair_ref = outs[1] if with_pair else None
        stage_body(
            step, plan, along, *refs[: 5 + len(tables) + len(slabs)], outs[0], pair_ref, *scratch
        )

    flops = sum(rows * per for present, rows in plan if present) * 100_000_000
    return pl.pallas_call(
        body,
        grid=(1,),
        out_shape=out_shape,
        in_specs=specs,
        out_specs=out_specs,
        scratch_shapes=[
            pltpu.VMEM((count,) + mine[0].shape, jnp.bfloat16),
            pltpu.VMEM((2, 2 * INNER, mine[0].shape[1]), jnp.float32),
            pltpu.VMEM((2 * count, INNER), jnp.float32),
            pltpu.VMEM((4 * INNER, 2 * mine[0].shape[1]), jnp.bfloat16),
            pltpu.VMEM((count, outer, INNER), jnp.float32),
            pltpu.SMEM((2 * count + 1,), jnp.int32),
            pltpu.SMEM((count,), jnp.int32),
            pltpu.SemaphoreType.DMA((count,)),
        ],
        input_output_aliases=aliases,
        cost_estimate=pl.CostEstimate(flops=flops, bytes_accessed=3_000_000, transcendentals=0),
        name=f"stage{step}",
    )(*args)


def finish_body(src_ref, own_w, own_ref, early_ref, late_ref, out_ref, lines):
    g = pl.program_id(0)
    first = early_ref.shape[0]
    outer = own_ref.shape[1]
    pitch = outer + 8
    for k in range(8):
        src = src_ref[g * 8 + k]
        live = own_w[g * 8 + k] != 0.0
        early = early_ref[jnp.clip(src, 0, first - 1)]
        late = late_ref[jnp.clip(src - first, 0, late_ref.shape[0] - 1)]
        value = jnp.where(src < 0, own_ref[k], jnp.where(src < first, early, late))
        lines[pl.ds(k * pitch, outer), :] = jnp.where(live, value, 0.0)
    for n in range(outer):
        out_ref[pl.ds(8 * n, 8), :] = lines[pl.ds(n, 8, stride=pitch), :]


def finish_call(src, own_w, own_buf, early, late):
    outer = LAGS // INNER
    total = src.shape[0]
    smem = pl.BlockSpec(memory_space=pltpu.SMEM)
    vmem = pl.BlockSpec(memory_space=pltpu.VMEM)
    return pl.pallas_call(
        finish_body,
        grid=(total // 8,),
        out_shape=jax.ShapeDtypeStruct((total * outer, INNER), jnp.float32),
        in_specs=[smem, smem, pl.BlockSpec((8, outer, INNER), lambda g: (g, 0, 0)), vmem, vmem],
        out_specs=pl.BlockSpec((8 * outer, INNER), lambda g: (g, 0)),
        scratch_shapes=[pltpu.VMEM((8 * (outer + 8), INNER), jnp.float32)],
        cost_estimate=pl.CostEstimate(flops=1_000_000, bytes_accessed=8_000_000, transcendentals=0),
        name="finish",
    )(src, own_w, own_buf, early, late)


def per_device(total, spectra, pair_mask, available):
    along = total // (ACROSS * CORES)
    far = along // 2
    freq = spectra.shape[2]
    column = 2 * freq // INNER
    tables = [jnp.asarray(table) for table in build_tables(freq)]

    def move(value, goal_of):
        pairs = []
        for start in range(total):
            x, z, c = start // (along * CORES), start // CORES % along, start % CORES
            x, z, c = goal_of(x, z, c)
            pairs.append((start, (x % ACROSS * along + z % along) * CORES + c % CORES))
        return lax.ppermute(value, "row", pairs)

    def swap(value):
        return move(value, lambda x, z, c: (x, z, c + 1))

    def onward(value):
        return move(value, lambda x, z, c: (x, z + 1 - 2 * c, c))

    def sideways(value):
        return move(value, lambda x, z, c: (x + 1 - 2 * c, z, c))

    me = lax.axis_index("row")
    x, z, c = me // (along * CORES), me // CORES % along, me % CORES
    info = jnp.stack([x, z, c]).astype(jnp.int32)

    own = fold_call(spectra.reshape(2 * freq // column, column))
    across = move(own, lambda x, z, c: (x + 2 - 4 * c, z, c))
    flag = lax.dynamic_slice_in_dim(available, me, 1, 0).astype(jnp.float32)
    own_w = pair_mask[0].astype(jnp.float32) * flag * available.astype(jnp.float32)
    pair_w = swap(own_w)
    other = swap(own)
    across, pair_w, other, info = lax.optimization_barrier((across, pair_w, other, info))
    slab = jnp.stack([own, across, other, swap(across)])
    mine = (own, other)

    cut = far - 2
    early = late = own_buf = side = None
    for step in range(far + 2):
        plan, slabs = [], []
        for value, stage in ((slab, step), (side, step - 1)):
            plan.append((value is not None, 2 if 0 < stage < far else 1))
            if value is not None:
                slabs.append(value)
        next_slab = onward(slab) if step < far else None
        side = sideways(slab) if step <= far else None
        paired = 1 <= step <= far
        if paired and step <= cut:
            buf, at, size = early, step - 1, 8 * cut
        elif paired:
            buf, at, size = late, step - 1 - cut, 8 * (far - cut)
        else:
            buf, at, size = None, None, None
        outs = stage_call(
            step, plan, along, slabs, info, own_w, pair_w, mine, tables, own_buf, buf, at, size
        )
        own_buf = outs[0]
        if paired and step <= cut:
            early = outs[1]
        elif paired:
            late = outs[1]
        slab = next_slab
        if step <= far:
            slab, side, own_buf, early, late = lax.optimization_barrier(
                (slab, side, own_buf, early, late)
            )
    early, late = swap(early), swap(late)

    j = lax.iota(jnp.int32, total)
    xj, zj, cj = j // (along * CORES), j // CORES % along, j % CORES
    dx, dz = (xj - x) % ACROSS, (zj - z) % along
    host = (dz < far).astype(jnp.int32)
    stage = jnp.where(dz < far, dz, along - dz)
    beside = dx % 2
    half = jnp.where(beside == 1, (dx + 1 - 2 * host) % ACROSS // 2, dx // 2)
    entry = 4 * beside + 2 * ((cj - host) % CORES) + half
    far_one = (host != c) & (dz != 0) & (dz != far)
    src = jnp.where(far_one, 8 * (stage - 1 + beside) + entry, -1).astype(jnp.int32)
    out = finish_call(src, own_w, own_buf, early, late)
    out = out.reshape(total // 8, LAGS // INNER, 8, INNER)
    return jnp.transpose(out, (0, 2, 1, 3)).reshape(1, total, LAGS)


def solution(mesh):
    return jax.shard_map(
        functools.partial(per_device, mesh.shape["row"]),
        mesh=mesh,
        in_specs=(P(("win", "row"), None, None), P("row", None), P("win")),
        out_specs=P(("win", "row"), None, None),
        check_vma=False,
    )
```

time: 508 us -> 159 us (0.31)
  local copies, waits for them, and re-layouts: 168 us -> 4.94 us
  waiting for transfers between devices: 168 us -> 7.95 us
  other arithmetic: 89.5 us -> 2.92 us
  Pallas kernels: 0 us -> 77.3 us
  matrix products: 66.9 us -> 0 us
  starting transfers between devices: 0.01 us -> 64.3 us
  between operations: 14.1 us -> 1.1 us
    all_gather x1 -> x0, waiting for transfers between devices: 167 us -> none  [per_device(): piece = lax.all_gather(spectra, 'row', axis=0, tiled=True)]
    pallas_call x0 -> x12, Pallas kernels: none -> 77.3 us  [the longest x10 64.1 us: stage_call(): pl.pallas_call(body, grid=(1,), out_shape=out_shape, in_specs=specs, out_...]
    dot_general x32 -> x0, matrix products: 66.9 us -> none  [the longest x16 34.5 us: pair_block(): jnp.einsum('uv,pvk->puk', section_one, cross, precision=lax.Precision.HIGH)]
    ppermute x0 -> x23, starting transfers between devices: none -> 64.3 us  [move(): return lax.ppermute(value, 'row', pairs)]
    reshape x16 -> x1, local copies, waits for them, and re-layouts: 64.5 us -> 1.63 us  [per_device(): own = fold_call(spectra.reshape(2 * freq // column, column))]
    another operation x16 -> x0, local copies, waits for them, and re-layouts: 47 us -> none  [pair_block(): jnp.stack([real_part, imag_part], axis=2)]
    dynamic_slice x17 -> x1, local copies, waits for them, and re-layouts: 32.5 us -> 1.24 us  [per_device(): flag = lax.dynamic_slice_in_dim(available, me, 1, 0).astype(jnp.float32)]
    slice x16 -> x0, other arithmetic: 24 us -> none  [pair_block(): return (2.0 * summed - real_part[:, :, :1]) * (1.0 / math.sqrt(8.0 * freq))]
  transfers between devices with their start and end apart: 1 -> 23, of which waited for: 1 -> 6; matrix products, arithmetic and copies ran while one was open for 1% -> 2% of each run, Pallas kernels for 0% -> 40%
where the time goes in v1:
time: 159 us
  Pallas kernels  77.3 us (49%)
  starting transfers between devices  64.3 us (40%)
  waiting for transfers between devices  7.95 us (5%)
  local copies, waits for them, and re-layouts  4.94 us (3%)
  other arithmetic  2.92 us (2%)
    ppermute x23, starting transfers between devices, move(): return lax.ppermute(value, 'row', pairs)  64.3 us
    pallas_call x10, Pallas kernels, stage_call(): pl.pallas_call(body, grid=(1,), out_shape=out_shape, in_specs=specs, out_...  64.1 us
    pallas_call x1, Pallas kernels, finish_call(): pl.pallas_call(finish_body, grid=(total // 8,), out_shape=jax.ShapeDtypeS...  11.5 us
    ppermute x23, waiting for transfers between devices, move(): return lax.ppermute(value, 'row', pairs)  7.95 us
  transfers between devices with their start and end apart: 23, of which 6 were waited for; matrix products, arithmetic and copies ran while one was open for 2% of the time, Pallas kernels for 40%

profile of v1, /device:TPU:33, one launch (start us, length us, event | category | flops | bytes accessed | tf_op | source)
XLA Modules:
  0.0 158.6 jit_solution(3549017920803661715)
XLA Ops:
  0.0 1.6 %reshape.12.whole_ref = bf16[128,512]{1,0:T(8,128)(2,1)} reshape(bf16[1,2,32768]{2,1,0:T(2,128)(2,1)} %param.7) | data formatting | bytes 262144 | tf_op jit(solution)/shard_map/reshape | solution.py:351
  1.6 1.8 %fold.1.refs_3_ = bf16[272,256]{1,0:T(8,128)(2,1)} custom-call(bf16[128,512]{1,0:T(8,128)(2,1)} %reshape.12.whole_ref), custom_call_target="tpu_custom_call" | custom-call | flops 1000000 | bytes 300000 | tf_op jit(solution)/shard_map/fold/pallas_call | solution.py:81
  3.4 20.4 %collective-permute-start.2 = (bf16[272,256]{1,0:T(8,128)(2,1)}, bf16[272,256]{1,0:T(8,128)(2,1)S(1)}, u32[]{:S(2)}, u32[]{:S(2)}) collective-permute-start(bf16[272,256]{1,0:T(8,128)(2,1)} %fold.1.refs_3_), channel_id=1, source_target_pairs={{0,1},{1,0},{2,3},{3,2},{4,5},{5,4},{6,7},{7,6},{8,9},{9,8},{10,11... | collective-permute-start | bytes 417800 | tf_op jit(solution)/shard_map/ppermute | solution.py:336
  23.8 1.2 dynamic_slice.3
  25.7 0.7 bitcast_multiply_fusion.refs_1_.own_w
  26.4 0.7 pad_add_fusion.refs_0_
  27.1 0.5 collective-permute-done.1.refs_2_
  27.6 3.2 %collective-permute-done = bf16[272,256]{1,0:T(8,128)(2,1)S(1)} collective-permute-done((bf16[272,256]{1,0:T(8,128)(2,1)}, bf16[272,256]{1,0:T(8,128)(2,1)S(1)}, u32[]{:S(2)}, u32[]{:S(2)}) %collective-permute-start) | collective-permute-done | bytes 139296 | tf_op jit(solution)/shard_map/ppermute | solution.py:336
  30.8 0.9 collective-permute-start.3
  31.6 1.0 collective-permute-done.3
  32.6 1.0 pad_maximum_fusion.refs_9_
  33.6 0.0 copy-start.2
  33.6 0.1 collective-permute-start.5
  33.7 6.0 %collective-permute-start.4 = (bf16[4,272,256]{2,1,0:T(8,128)(2,1)S(1)}, bf16[4,272,256]{2,1,0:T(8,128)(2,1)S(1)}, u32[]{:S(2)}, u32[]{:S(2)}) collective-permute-start(bf16[4,272,256]{2,1,0:T(8,128)(2,1)S(1)} %pad_maximum_fusion.refs_9_), channel_id=1, source_target_pairs={{0,2},{1,31},{2,4},{3,1},{4,6},{5,3},{6,8},{7,5},{8,10},{9,7},{10,... | collective-permute-start | bytes 1671176 | tf_op jit(solution)/shard_map/ppermute | solution.py:336
  39.7 3.5 %stage0.1.refs_11_ = f32[128,64,128]{2,1,0:T(8,128)} custom-call(s32[3]{0:T(128)} %pad_add_fusion.refs_0_, f32[128]{0:T(128)} %copy-done.21, f32[128]{0:T(128)} %copy-done.22, bf16[272,256]{1,0:T(8,128)(2,1)} %fold.1.refs_3_, bf16[272,256]{1,0:T(8,128)(2,1)} %copy-done.1, bf16[512,256]{1,0:T(8,128)(2,1)} %constant.149.clone.refs_5_, ...), custom_call_target="tpu_custom_call" | custom-call | flops 400000000 | bytes 3000000 | tf_op jit(solution)/shard_map/stage0/pallas_call | solution.py:268
  43.3 2.9 %collective-permute-done.4.refs_9_ = bf16[4,272,256]{2,1,0:T(8,128)(2,1)S(1)} collective-permute-done((bf16[4,272,256]{2,1,0:T(8,128)(2,1)S(1)}, bf16[4,272,256]{2,1,0:T(8,128)(2,1)S(1)}, u32[]{:S(2)}, u32[]{:S(2)}) %collective-permute-start.4) | collective-permute-done | bytes 557088 | tf_op jit(solution)/shard_map/ppermute | solution.py:336
  46.2 0.4 collective-permute-start.7
  46.6 3.1 %collective-permute-start.6 = (bf16[4,272,256]{2,1,0:T(8,128)(2,1)S(1)}, bf16[4,272,256]{2,1,0:T(8,128)(2,1)S(1)}, u32[]{:S(2)}, u32[]{:S(2)}) collective-permute-start(bf16[4,272,256]{2,1,0:T(8,128)(2,1)S(1)} %collective-permute-done.4.refs_9_), channel_id=1, source_target_pairs={{0,2},{1,31},{2,4},{3,1},{4,6},{5,3},{6,8},{7,5},{8,10},{9,7},{10,... | collective-permute-start | bytes 1671176 | tf_op jit(solution)/shard_map/ppermute | solution.py:336
  49.7 7.0 %stage1.1 = (f32[128,64,128]{2,1,0:T(8,128)}, f32[48,64,128]{2,1,0:T(8,128)}) custom-call(s32[3]{0:T(128)} %pad_add_fusion.refs_0_, f32[128]{0:T(128)} %copy-done.21, f32[128]{0:T(128)} %copy-done.22, bf16[272,256]{1,0:T(8,128)(2,1)} %fold.1.refs_3_, bf16[272,256]{1,0:T(8,128)(2,1)} %copy-done.1, ...), custom_call_target="tpu_custom_call", output_to_operand_aliasing={{0}: (11, {})} | custom-call | flops 1200000000 | bytes 3000000 | tf_op jit(solution)/shard_map/stage1/pallas_call | solution.py:268
  56.8 0.1 collective-permute-start.9
  56.9 2.5 %collective-permute-start.8 = (bf16[4,272,256]{2,1,0:T(8,128)(2,1)S(1)}, bf16[4,272,256]{2,1,0:T(8,128)(2,1)S(1)}, u32[]{:S(2)}, u32[]{:S(2)}) collective-permute-start(bf16[4,272,256]{2,1,0:T(8,128)(2,1)S(1)} %collective-permute-done.6.refs_9_), channel_id=1, source_target_pairs={{0,2},{1,31},{2,4},{3,1},{4,6},{5,3},{6,8},{7,5},{8,10},{9,7},{10,... | collective-permute-start | bytes 1671176 | tf_op jit(solution)/shard_map/ppermute | solution.py:336
  59.5 7.6 %stage2.1 = (f32[128,64,128]{2,1,0:T(8,128)}, f32[48,64,128]{2,1,0:T(8,128)}) custom-call(s32[3]{0:T(128)} %pad_add_fusion.refs_0_, f32[128]{0:T(128)} %copy-done.21, f32[128]{0:T(128)} %copy-done.22, bf16[272,256]{1,0:T(8,128)(2,1)} %fold.1.refs_3_, bf16[272,256]{1,0:T(8,128)(2,1)} %copy-done.1, ...), custom_call_target="tpu_custom_call", output_to_operand_aliasing={{0}: (11, {}), {1}: (12, {})} | custom-call | flops 1600000000 | bytes 3000000 | tf_op jit(solution)/shard_map/stage2/pallas_call | solution.py:268
  67.1 0.1 collective-permute-start.11
  67.3 2.1 %collective-permute-start.10 = (bf16[4,272,256]{2,1,0:T(8,128)(2,1)S(1)}, bf16[4,272,256]{2,1,0:T(8,128)(2,1)S(1)}, u32[]{:S(2)}, u32[]{:S(2)}) collective-permute-start(bf16[4,272,256]{2,1,0:T(8,128)(2,1)S(1)} %collective-permute-done.8.refs_9_), channel_id=1, source_target_pairs={{0,2},{1,31},{2,4},{3,1},{4,6},{5,3},{6,8},{7,5},{8,10},{9,7},{10,... | collective-permute-start | bytes 1671176 | tf_op jit(solution)/shard_map/ppermute | solution.py:336
  69.4 7.1 %stage3.1 = (f32[128,64,128]{2,1,0:T(8,128)}, f32[48,64,128]{2,1,0:T(8,128)}) custom-call(s32[3]{0:T(128)} %pad_add_fusion.refs_0_, f32[128]{0:T(128)} %copy-done.21, f32[128]{0:T(128)} %copy-done.22, bf16[272,256]{1,0:T(8,128)(2,1)} %fold.1.refs_3_, bf16[272,256]{1,0:T(8,128)(2,1)} %copy-done.1, ...), custom_call_target="tpu_custom_call", output_to_operand_aliasing={{0}: (11, {}), {1}: (12, {})} | custom-call | flops 1600000000 | bytes 3000000 | tf_op jit(solution)/shard_map/stage3/pallas_call | solution.py:268
  76.6 2.0 %collective-permute-start.13 = (bf16[4,272,256]{2,1,0:T(8,128)(2,1)S(1)}, bf16[4,272,256]{2,1,0:T(8,128)(2,1)S(1)}, u32[]{:S(2)}, u32[]{:S(2)}) collective-permute-start(bf16[4,272,256]{2,1,0:T(8,128)(2,1)S(1)} %collective-permute-done.10.refs_9_), channel_id=1, source_target_pairs={{0,32},{1,97},{2,34},{3,99},{4,36},{5,101},{6,38},{7,103},{8,40},{... | collective-permute-start | bytes 1671176 | tf_op jit(solution)/shard_map/ppermute | solution.py:336
  78.5 3.1 %collective-permute-start.12 = (bf16[4,272,256]{2,1,0:T(8,128)(2,1)S(1)}, bf16[4,272,256]{2,1,0:T(8,128)(2,1)S(1)}, u32[]{:S(2)}, u32[]{:S(2)}) collective-permute-start(bf16[4,272,256]{2,1,0:T(8,128)(2,1)S(1)} %collective-permute-done.10.refs_9_), channel_id=1, source_target_pairs={{0,2},{1,31},{2,4},{3,1},{4,6},{5,3},{6,8},{7,5},{8,10},{9,7},{10,... | collective-permute-start | bytes 1671176 | tf_op jit(solution)/shard_map/ppermute | solution.py:336
  81.6 7.6 %stage4.1 = (f32[128,64,128]{2,1,0:T(8,128)}, f32[48,64,128]{2,1,0:T(8,128)}) custom-call(s32[3]{0:T(128)} %pad_add_fusion.refs_0_, f32[128]{0:T(128)} %copy-done.21, f32[128]{0:T(128)} %copy-done.22, bf16[272,256]{1,0:T(8,128)(2,1)} %fold.1.refs_3_, bf16[272,256]{1,0:T(8,128)(2,1)} %copy-done.1, ...), custom_call_target="tpu_custom_call", output_to_operand_aliasing={{0}: (11, {}), {1}: (12, {})} | custom-call | flops 1600000000 | bytes 3000000 | tf_op jit(solution)/shard_map/stage4/pallas_call | solution.py:268
  89.3 0.1 collective-permute-start.15
  89.5 2.2 %collective-permute-start.14 = (bf16[4,272,256]{2,1,0:T(8,128)(2,1)S(1)}, bf16[4,272,256]{2,1,0:T(8,128)(2,1)S(1)}, u32[]{:S(2)}, u32[]{:S(2)}) collective-permute-start(bf16[4,272,256]{2,1,0:T(8,128)(2,1)S(1)} %collective-permute-done.12.refs_9_), channel_id=1, source_target_pairs={{0,2},{1,31},{2,4},{3,1},{4,6},{5,3},{6,8},{7,5},{8,10},{9,7},{10,... | collective-permute-start | bytes 1671176 | tf_op jit(solution)/shard_map/ppermute | solution.py:336
  91.7 7.1 %stage5.1 = (f32[128,64,128]{2,1,0:T(8,128)}, f32[48,64,128]{2,1,0:T(8,128)}) custom-call(s32[3]{0:T(128)} %pad_add_fusion.refs_0_, f32[128]{0:T(128)} %copy-done.21, f32[128]{0:T(128)} %copy-done.22, bf16[272,256]{1,0:T(8,128)(2,1)} %fold.1.refs_3_, bf16[272,256]{1,0:T(8,128)(2,1)} %copy-done.1, ...), custom_call_target="tpu_custom_call", output_to_operand_aliasing={{0}: (11, {}), {1}: (12, {})} | custom-call | flops 1600000000 | bytes 3000000 | tf_op jit(solution)/shard_map/stage5/pallas_call | solution.py:268
  98.8 0.3 collective-permute-start.17
  99.2 2.5 %collective-permute-start.16 = (bf16[4,272,256]{2,1,0:T(8,128)(2,1)S(1)}, bf16[4,272,256]{2,1,0:T(8,128)(2,1)S(1)}, u32[]{:S(2)}, u32[]{:S(2)}) collective-permute-start(bf16[4,272,256]{2,1,0:T(8,128)(2,1)S(1)} %collective-permute-done.14.refs_9_), channel_id=1, source_target_pairs={{0,2},{1,31},{2,4},{3,1},{4,6},{5,3},{6,8},{7,5},{8,10},{9,7},{10,... | collective-permute-start | bytes 1671176 | tf_op jit(solution)/shard_map/ppermute | solution.py:336
  101.7 7.1 %stage6.1 = (f32[128,64,128]{2,1,0:T(8,128)}, f32[48,64,128]{2,1,0:T(8,128)}) custom-call(s32[3]{0:T(128)} %pad_add_fusion.refs_0_, f32[128]{0:T(128)} %copy-done.21, f32[128]{0:T(128)} %copy-done.22, bf16[272,256]{1,0:T(8,128)(2,1)} %fold.1.refs_3_, bf16[272,256]{1,0:T(8,128)(2,1)} %copy-done.1, ...), custom_call_target="tpu_custom_call", output_to_operand_aliasing={{0}: (11, {}), {1}: (12, {})} | custom-call | flops 1600000000 | bytes 3000000 | tf_op jit(solution)/shard_map/stage6/pallas_call | solution.py:268
  108.8 0.1 collective-permute-start.19
  109.0 2.6 %collective-permute-start.18 = (bf16[4,272,256]{2,1,0:T(8,128)(2,1)S(1)}, bf16[4,272,256]{2,1,0:T(8,128)(2,1)S(1)}, u32[]{:S(2)}, u32[]{:S(2)}) collective-permute-start(bf16[4,272,256]{2,1,0:T(8,128)(2,1)S(1)} %collective-permute-done.16.refs_9_), channel_id=1, source_target_pairs={{0,2},{1,31},{2,4},{3,1},{4,6},{5,3},{6,8},{7,5},{8,10},{9,7},{10,... | collective-permute-start | bytes 1671176 | tf_op jit(solution)/shard_map/ppermute | solution.py:336
  111.6 6.3 %stage7.1 = (f32[128,64,128]{2,1,0:T(8,128)}, f32[16,64,128]{2,1,0:T(8,128)}) custom-call(s32[3]{0:T(128)} %pad_add_fusion.refs_0_, f32[128]{0:T(128)} %copy-done.21, f32[128]{0:T(128)} %copy-done.22, bf16[272,256]{1,0:T(8,128)(2,1)} %fold.1.refs_3_, bf16[272,256]{1,0:T(8,128)(2,1)} %copy-done.1, ...), custom_call_target="tpu_custom_call", output_to_operand_aliasing={{0}: (11, {})} | custom-call | flops 1600000000 | bytes 3000000 | tf_op jit(solution)/shard_map/stage7/pallas_call | solution.py:268
  117.9 0.0 copy-start
  118.0 0.1 collective-permute-done.18.refs_9_
  118.1 2.7 %collective-permute-start.20 = (bf16[4,272,256]{2,1,0:T(8,128)(2,1)S(1)}, bf16[4,272,256]{2,1,0:T(8,128)(2,1)S(1)}, u32[]{:S(2)}, u32[]{:S(2)}) collective-permute-start(bf16[4,272,256]{2,1,0:T(8,128)(2,1)S(1)} %collective-permute-done.18.refs_9_), channel_id=1, source_target_pairs={{0,32},{1,97},{2,34},{3,99},{4,36},{5,101},{6,38},{7,103},{8,40},{... | collective-permute-start | bytes 1671176 | tf_op jit(solution)/shard_map/ppermute | solution.py:336
  120.7 6.5 %stage8.1 = (f32[128,64,128]{2,1,0:T(8,128)}, f32[16,64,128]{2,1,0:T(8,128)}) custom-call(s32[3]{0:T(128)} %pad_add_fusion.refs_0_, f32[128]{0:T(128)} %copy-done.21, f32[128]{0:T(128)} %copy-done.22, bf16[272,256]{1,0:T(8,128)(2,1)} %fold.1.refs_3_, bf16[272,256]{1,0:T(8,128)(2,1)} %copy-done.1, ...), custom_call_target="tpu_custom_call", output_to_operand_aliasing={{0}: (11, {}), {1}: (12, {})} | custom-call | flops 1200000000 | bytes 3000000 | tf_op jit(solution)/shard_map/stage8/pallas_call | solution.py:268
  127.2 0.3 collective-permute-done.20.refs_9_
  127.5 0.8 copy-done.20
  128.3 12.8 %collective-permute-start.21 = (f32[48,64,128]{2,1,0:T(8,128)S(1)}, f32[48,64,128]{2,1,0:T(8,128)S(1)}, u32[]{:S(2)}, u32[]{:S(2)}) collective-permute-start(f32[48,64,128]{2,1,0:T(8,128)S(1)} %copy-done), channel_id=1, source_target_pairs={{0,1},{1,0},{2,3},{3,2},{4,5},{5,4},{6,7},{7,6},{8,9},{9,8},{10,11... | collective-permute-start | bytes 4718600 | tf_op jit(solution)/shard_map/ppermute | solution.py:336
  141.2 0.6 and_select_fusion.8.src_ref
  141.8 4.2 %stage9.1.own_ref = f32[128,64,128]{2,1,0:T(8,128)} custom-call(s32[3]{0:T(128)} %pad_add_fusion.refs_0_, f32[128]{0:T(128)} %copy-done.21, f32[128]{0:T(128)} %copy-done.22, bf16[272,256]{1,0:T(8,128)(2,1)} %fold.1.refs_3_, bf16[272,256]{1,0:T(8,128)(2,1)} %copy-done.1, bf16[512,256]{1,0:T(8,128)(2,1)} %constant.149.clone.refs_5_, ...), custom_call_target="tpu_custom_call", output_to_operand_aliasing={{}: (10, {})} | custom-call | flops 400000000 | bytes 3000000 | tf_op jit(solution)/shard_map/stage9/pallas_call | solution.py:268
  146.0 1.2 copy-done.3
  147.1 11.5 %finish.1 = f32[8192,128]{1,0:T(8,128)} custom-call(s32[128]{0:T(128)} %and_select_fusion.8.src_ref, f32[128]{0:T(128)} %copy-done.21, f32[128,64,128]{2,1,0:T(8,128)} %stage9.1.own_ref, f32[48,64,128]{2,1,0:T(8,128)} %copy-done.3, f32[16,64,128]{2,1,0:T(8,128)} %collective-permute-done.22.late_ref), custom_call_target="tpu_custom_call" | custom-call | flops 1000000 | bytes 8000000 | tf_op jit(solution)/shard_map/finish/pallas_call | solution.py:311
  (62 shorter events, 0.1 us)
Async XLA Ops:
  3.4 24.2 %collective-permute-start.2 = (bf16[272,256]{1,0:T(8,128)(2,1)}, bf16[272,256]{1,0:T(8,128)(2,1)S(1)}, u32[]{:S(2)}, u32[]{:S(2)}) collective-permute-start(bf16[272,256]{1,0:T(8,128)(2,1)} %fold.1.refs_3_), channel_id=1, source_target_pairs={{0,1},{1,0},{2,3},{3,2},{4,5},{5,4},{6,7},{7,6},{8,9},{9,8},{10,11... | collective-permute-start | bytes 417800 | tf_op jit(solution)/shard_map/ppermute | solution.py:336
  23.8 6.9 %collective-permute-start = (bf16[272,256]{1,0:T(8,128)(2,1)}, bf16[272,256]{1,0:T(8,128)(2,1)S(1)}, u32[]{:S(2)}, u32[]{:S(2)}) collective-permute-start(bf16[272,256]{1,0:T(8,128)(2,1)} %fold.1.refs_3_), channel_id=1, source_target_pairs={{0,64},{1,65},{2,66},{3,67},{4,68},{5,69},{6,70},{7,71},{8,72},{9,... | collective-permute-start | bytes 417800 | tf_op jit(solution)/shard_map/ppermute | solution.py:336
  26.4 13.3 %copy-start.21 = (f32[128]{0:T(128)}, f32[128]{0:T(128)S(1)}, u32[]{:S(2)}) copy-start(f32[128]{0:T(128)S(1)} %bitcast_multiply_fusion.refs_1_.own_w) | copy-start | bytes 1540
  26.4 1.2 collective-permute-start.1
  27.6 12.2 %copy-start.22 = (f32[128]{0:T(128)}, f32[128]{0:T(128)S(1)}, u32[]{:S(2)}) copy-start(f32[128]{0:T(128)S(1)} %collective-permute-done.1.refs_2_) | copy-start | bytes 1540
  27.6 12.2 %copy-start.1 = (bf16[272,256]{1,0:T(8,128)(2,1)}, bf16[272,256]{1,0:T(8,128)(2,1)S(1)}, u32[]{:S(2)}) copy-start(bf16[272,256]{1,0:T(8,128)(2,1)S(1)} %collective-permute-done.2.refs_4_) | copy-start | bytes 417796
  30.8 1.9 %collective-permute-start.3 = (bf16[272,256]{1,0:T(8,128)(2,1)S(1)}, bf16[272,256]{1,0:T(8,128)(2,1)S(1)}, u32[]{:S(2)}, u32[]{:S(2)}) collective-permute-start(bf16[272,256]{1,0:T(8,128)(2,1)S(1)} %collective-permute-done), channel_id=1, source_target_pairs={{0,1},{1,0},{2,3},{3,2},{4,5},{5,4},{6,7},{7,6},{8,9},{9,8},{10,11... | collective-permute-start | bytes 417800 | tf_op jit(solution)/shard_map/ppermute | solution.py:336
  33.6 6.1 %copy-start.2 = (bf16[4,272,256]{2,1,0:T(8,128)(2,1)}, bf16[4,272,256]{2,1,0:T(8,128)(2,1)S(1)}, u32[]{:S(2)}) copy-start(bf16[4,272,256]{2,1,0:T(8,128)(2,1)S(1)} %pad_maximum_fusion.refs_9_) | copy-start | bytes 1671172
  33.6 9.7 %collective-permute-start.5 = (bf16[4,272,256]{2,1,0:T(8,128)(2,1)S(1)}, bf16[4,272,256]{2,1,0:T(8,128)(2,1)S(1)}, u32[]{:S(2)}, u32[]{:S(2)}) collective-permute-start(bf16[4,272,256]{2,1,0:T(8,128)(2,1)S(1)} %pad_maximum_fusion.refs_9_), channel_id=1, source_target_pairs={{0,32},{1,97},{2,34},{3,99},{4,36},{5,101},{6,38},{7,103},{8,40},{... | collective-permute-start | bytes 1671176 | tf_op jit(solution)/shard_map/ppermute | solution.py:336
  33.7 12.4 %collective-permute-start.4 = (bf16[4,272,256]{2,1,0:T(8,128)(2,1)S(1)}, bf16[4,272,256]{2,1,0:T(8,128)(2,1)S(1)}, u32[]{:S(2)}, u32[]{:S(2)}) collective-permute-start(bf16[4,272,256]{2,1,0:T(8,128)(2,1)S(1)} %pad_maximum_fusion.refs_9_), channel_id=1, source_target_pairs={{0,2},{1,31},{2,4},{3,1},{4,6},{5,3},{6,8},{7,5},{8,10},{9,7},{10,... | collective-permute-start | bytes 1671176 | tf_op jit(solution)/shard_map/ppermute | solution.py:336
  43.3 6.4 %copy-start.19 = (bf16[4,272,256]{2,1,0:T(8,128)(2,1)}, bf16[4,272,256]{2,1,0:T(8,128)(2,1)S(1)}, u32[]{:S(2)}) copy-start(bf16[4,272,256]{2,1,0:T(8,128)(2,1)S(1)} %collective-permute-done.5.refs_10_) | copy-start | bytes 1671172
  46.2 3.5 %copy-start.18 = (bf16[4,272,256]{2,1,0:T(8,128)(2,1)}, bf16[4,272,256]{2,1,0:T(8,128)(2,1)S(1)}, u32[]{:S(2)}) copy-start(bf16[4,272,256]{2,1,0:T(8,128)(2,1)S(1)} %collective-permute-done.4.refs_9_) | copy-start | bytes 1671172
  46.2 10.5 %collective-permute-start.7 = (bf16[4,272,256]{2,1,0:T(8,128)(2,1)S(1)}, bf16[4,272,256]{2,1,0:T(8,128)(2,1)S(1)}, u32[]{:S(2)}, u32[]{:S(2)}) collective-permute-start(bf16[4,272,256]{2,1,0:T(8,128)(2,1)S(1)} %collective-permute-done.4.refs_9_), channel_id=1, source_target_pairs={{0,32},{1,97},{2,34},{3,99},{4,36},{5,101},{6,38},{7,103},{8,40},{... | collective-permute-start | bytes 1671176 | tf_op jit(solution)/shard_map/ppermute | solution.py:336
  46.6 10.1 %collective-permute-start.6 = (bf16[4,272,256]{2,1,0:T(8,128)(2,1)S(1)}, bf16[4,272,256]{2,1,0:T(8,128)(2,1)S(1)}, u32[]{:S(2)}, u32[]{:S(2)}) collective-permute-start(bf16[4,272,256]{2,1,0:T(8,128)(2,1)S(1)} %collective-permute-done.4.refs_9_), channel_id=1, source_target_pairs={{0,2},{1,31},{2,4},{3,1},{4,6},{5,3},{6,8},{7,5},{8,10},{9,7},{10,... | collective-permute-start | bytes 1671176 | tf_op jit(solution)/shard_map/ppermute | solution.py:336
  56.7 2.7 %copy-start.13 = (bf16[4,272,256]{2,1,0:T(8,128)(2,1)}, bf16[4,272,256]{2,1,0:T(8,128)(2,1)S(1)}, u32[]{:S(2)}) copy-start(bf16[4,272,256]{2,1,0:T(8,128)(2,1)S(1)} %collective-permute-done.7.refs_10_) | copy-start | bytes 1671172
  56.8 2.7 %copy-start.8 = (bf16[4,272,256]{2,1,0:T(8,128)(2,1)}, bf16[4,272,256]{2,1,0:T(8,128)(2,1)S(1)}, u32[]{:S(2)}) copy-start(bf16[4,272,256]{2,1,0:T(8,128)(2,1)S(1)} %collective-permute-done.6.refs_9_) | copy-start | bytes 1671172
  56.8 10.3 %collective-permute-start.9 = (bf16[4,272,256]{2,1,0:T(8,128)(2,1)S(1)}, bf16[4,272,256]{2,1,0:T(8,128)(2,1)S(1)}, u32[]{:S(2)}, u32[]{:S(2)}) collective-permute-start(bf16[4,272,256]{2,1,0:T(8,128)(2,1)S(1)} %collective-permute-done.6.refs_9_), channel_id=1, source_target_pairs={{0,32},{1,97},{2,34},{3,99},{4,36},{5,101},{6,38},{7,103},{8,40},{... | collective-permute-start | bytes 1671176 | tf_op jit(solution)/shard_map/ppermute | solution.py:336
  56.9 10.2 %collective-permute-start.8 = (bf16[4,272,256]{2,1,0:T(8,128)(2,1)S(1)}, bf16[4,272,256]{2,1,0:T(8,128)(2,1)S(1)}, u32[]{:S(2)}, u32[]{:S(2)}) collective-permute-start(bf16[4,272,256]{2,1,0:T(8,128)(2,1)S(1)} %collective-permute-done.6.refs_9_), channel_id=1, source_target_pairs={{0,2},{1,31},{2,4},{3,1},{4,6},{5,3},{6,8},{7,5},{8,10},{9,7},{10,... | collective-permute-start | bytes 1671176 | tf_op jit(solution)/shard_map/ppermute | solution.py:336
  67.1 2.3 %copy-start.9 = (bf16[4,272,256]{2,1,0:T(8,128)(2,1)}, bf16[4,272,256]{2,1,0:T(8,128)(2,1)S(1)}, u32[]{:S(2)}) copy-start(bf16[4,272,256]{2,1,0:T(8,128)(2,1)S(1)} %collective-permute-done.9.refs_10_) | copy-start | bytes 1671172
  67.1 2.2 %copy-start.4 = (bf16[4,272,256]{2,1,0:T(8,128)(2,1)}, bf16[4,272,256]{2,1,0:T(8,128)(2,1)S(1)}, u32[]{:S(2)}) copy-start(bf16[4,272,256]{2,1,0:T(8,128)(2,1)S(1)} %collective-permute-done.8.refs_9_) | copy-start | bytes 1671172
  67.1 9.4 %collective-permute-start.11 = (bf16[4,272,256]{2,1,0:T(8,128)(2,1)S(1)}, bf16[4,272,256]{2,1,0:T(8,128)(2,1)S(1)}, u32[]{:S(2)}, u32[]{:S(2)}) collective-permute-start(bf16[4,272,256]{2,1,0:T(8,128)(2,1)S(1)} %collective-permute-done.8.refs_9_), channel_id=1, source_target_pairs={{0,32},{1,97},{2,34},{3,99},{4,36},{5,101},{6,38},{7,103},{8,40},{... | collective-permute-start | bytes 1671176 | tf_op jit(solution)/shard_map/ppermute | solution.py:336
  67.3 9.3 %collective-permute-start.10 = (bf16[4,272,256]{2,1,0:T(8,128)(2,1)S(1)}, bf16[4,272,256]{2,1,0:T(8,128)(2,1)S(1)}, u32[]{:S(2)}, u32[]{:S(2)}) collective-permute-start(bf16[4,272,256]{2,1,0:T(8,128)(2,1)S(1)} %collective-permute-done.8.refs_9_), channel_id=1, source_target_pairs={{0,2},{1,31},{2,4},{3,1},{4,6},{5,3},{6,8},{7,5},{8,10},{9,7},{10,... | collective-permute-start | bytes 1671176 | tf_op jit(solution)/shard_map/ppermute | solution.py:336
  76.5 5.1 %copy-start.10 = (bf16[4,272,256]{2,1,0:T(8,128)(2,1)}, bf16[4,272,256]{2,1,0:T(8,128)(2,1)S(1)}, u32[]{:S(2)}) copy-start(bf16[4,272,256]{2,1,0:T(8,128)(2,1)S(1)} %collective-permute-done.11.refs_10_) | copy-start | bytes 1671172
  76.5 5.1 %copy-start.5 = (bf16[4,272,256]{2,1,0:T(8,128)(2,1)}, bf16[4,272,256]{2,1,0:T(8,128)(2,1)S(1)}, u32[]{:S(2)}) copy-start(bf16[4,272,256]{2,1,0:T(8,128)(2,1)S(1)} %collective-permute-done.10.refs_9_) | copy-start | bytes 1671172
  76.6 12.7 %collective-permute-start.13 = (bf16[4,272,256]{2,1,0:T(8,128)(2,1)S(1)}, bf16[4,272,256]{2,1,0:T(8,128)(2,1)S(1)}, u32[]{:S(2)}, u32[]{:S(2)}) collective-permute-start(bf16[4,272,256]{2,1,0:T(8,128)(2,1)S(1)} %collective-permute-done.10.refs_9_), channel_id=1, source_target_pairs={{0,32},{1,97},{2,34},{3,99},{4,36},{5,101},{6,38},{7,103},{8,40},{... | collective-permute-start | bytes 1671176 | tf_op jit(solution)/shard_map/ppermute | solution.py:336
  78.5 10.8 %collective-permute-start.12 = (bf16[4,272,256]{2,1,0:T(8,128)(2,1)S(1)}, bf16[4,272,256]{2,1,0:T(8,128)(2,1)S(1)}, u32[]{:S(2)}, u32[]{:S(2)}) collective-permute-start(bf16[4,272,256]{2,1,0:T(8,128)(2,1)S(1)} %collective-permute-done.10.refs_9_), channel_id=1, source_target_pairs={{0,2},{1,31},{2,4},{3,1},{4,6},{5,3},{6,8},{7,5},{8,10},{9,7},{10,... | collective-permute-start | bytes 1671176 | tf_op jit(solution)/shard_map/ppermute | solution.py:336
  89.3 2.4 %copy-start.11 = (bf16[4,272,256]{2,1,0:T(8,128)(2,1)}, bf16[4,272,256]{2,1,0:T(8,128)(2,1)S(1)}, u32[]{:S(2)}) copy-start(bf16[4,272,256]{2,1,0:T(8,128)(2,1)S(1)} %collective-permute-done.13.refs_10_) | copy-start | bytes 1671172
  89.3 2.3 %copy-start.6 = (bf16[4,272,256]{2,1,0:T(8,128)(2,1)}, bf16[4,272,256]{2,1,0:T(8,128)(2,1)S(1)}, u32[]{:S(2)}) copy-start(bf16[4,272,256]{2,1,0:T(8,128)(2,1)S(1)} %collective-permute-done.12.refs_9_) | copy-start | bytes 1671172
  89.3 9.5 %collective-permute-start.15 = (bf16[4,272,256]{2,1,0:T(8,128)(2,1)S(1)}, bf16[4,272,256]{2,1,0:T(8,128)(2,1)S(1)}, u32[]{:S(2)}, u32[]{:S(2)}) collective-permute-start(bf16[4,272,256]{2,1,0:T(8,128)(2,1)S(1)} %collective-permute-done.12.refs_9_), channel_id=1, source_target_pairs={{0,32},{1,97},{2,34},{3,99},{4,36},{5,101},{6,38},{7,103},{8,40},{... | collective-permute-start | bytes 1671176 | tf_op jit(solution)/shard_map/ppermute | solution.py:336
  89.5 9.4 %collective-permute-start.14 = (bf16[4,272,256]{2,1,0:T(8,128)(2,1)S(1)}, bf16[4,272,256]{2,1,0:T(8,128)(2,1)S(1)}, u32[]{:S(2)}, u32[]{:S(2)}) collective-permute-start(bf16[4,272,256]{2,1,0:T(8,128)(2,1)S(1)} %collective-permute-done.12.refs_9_), channel_id=1, source_target_pairs={{0,2},{1,31},{2,4},{3,1},{4,6},{5,3},{6,8},{7,5},{8,10},{9,7},{10,... | collective-permute-start | bytes 1671176 | tf_op jit(solution)/shard_map/ppermute | solution.py:336
  98.8 2.9 %copy-start.12 = (bf16[4,272,256]{2,1,0:T(8,128)(2,1)}, bf16[4,272,256]{2,1,0:T(8,128)(2,1)S(1)}, u32[]{:S(2)}) copy-start(bf16[4,272,256]{2,1,0:T(8,128)(2,1)S(1)} %collective-permute-done.15.refs_10_) | copy-start | bytes 1671172
  98.8 2.9 %copy-start.7 = (bf16[4,272,256]{2,1,0:T(8,128)(2,1)}, bf16[4,272,256]{2,1,0:T(8,128)(2,1)S(1)}, u32[]{:S(2)}) copy-start(bf16[4,272,256]{2,1,0:T(8,128)(2,1)S(1)} %collective-permute-done.14.refs_9_) | copy-start | bytes 1671172
  98.8 9.9 %collective-permute-start.17 = (bf16[4,272,256]{2,1,0:T(8,128)(2,1)S(1)}, bf16[4,272,256]{2,1,0:T(8,128)(2,1)S(1)}, u32[]{:S(2)}, u32[]{:S(2)}) collective-permute-start(bf16[4,272,256]{2,1,0:T(8,128)(2,1)S(1)} %collective-permute-done.14.refs_9_), channel_id=1, source_target_pairs={{0,32},{1,97},{2,34},{3,99},{4,36},{5,101},{6,38},{7,103},{8,40},{... | collective-permute-start | bytes 1671176 | tf_op jit(solution)/shard_map/ppermute | solution.py:336
  99.2 9.6 %collective-permute-start.16 = (bf16[4,272,256]{2,1,0:T(8,128)(2,1)S(1)}, bf16[4,272,256]{2,1,0:T(8,128)(2,1)S(1)}, u32[]{:S(2)}, u32[]{:S(2)}) collective-permute-start(bf16[4,272,256]{2,1,0:T(8,128)(2,1)S(1)} %collective-permute-done.14.refs_9_), channel_id=1, source_target_pairs={{0,2},{1,31},{2,4},{3,1},{4,6},{5,3},{6,8},{7,5},{8,10},{9,7},{10,... | collective-permute-start | bytes 1671176 | tf_op jit(solution)/shard_map/ppermute | solution.py:336
  108.8 2.8 %copy-start.17 = (bf16[4,272,256]{2,1,0:T(8,128)(2,1)}, bf16[4,272,256]{2,1,0:T(8,128)(2,1)S(1)}, u32[]{:S(2)}) copy-start(bf16[4,272,256]{2,1,0:T(8,128)(2,1)S(1)} %collective-permute-done.17.refs_10_) | copy-start | bytes 1671172
  108.8 2.8 %copy-start.16 = (bf16[4,272,256]{2,1,0:T(8,128)(2,1)}, bf16[4,272,256]{2,1,0:T(8,128)(2,1)S(1)}, u32[]{:S(2)}) copy-start(bf16[4,272,256]{2,1,0:T(8,128)(2,1)S(1)} %collective-permute-done.16.refs_9_) | copy-start | bytes 1671172
  108.8 9.1 %collective-permute-start.19 = (bf16[4,272,256]{2,1,0:T(8,128)(2,1)S(1)}, bf16[4,272,256]{2,1,0:T(8,128)(2,1)S(1)}, u32[]{:S(2)}, u32[]{:S(2)}) collective-permute-start(bf16[4,272,256]{2,1,0:T(8,128)(2,1)S(1)} %collective-permute-done.16.refs_9_), channel_id=1, source_target_pairs={{0,32},{1,97},{2,34},{3,99},{4,36},{5,101},{6,38},{7,103},{8,40},{... | collective-permute-start | bytes 1671176 | tf_op jit(solution)/shard_map/ppermute | solution.py:336
  109.0 9.1 %collective-permute-start.18 = (bf16[4,272,256]{2,1,0:T(8,128)(2,1)S(1)}, bf16[4,272,256]{2,1,0:T(8,128)(2,1)S(1)}, u32[]{:S(2)}, u32[]{:S(2)}) collective-permute-start(bf16[4,272,256]{2,1,0:T(8,128)(2,1)S(1)} %collective-permute-done.16.refs_9_), channel_id=1, source_target_pairs={{0,2},{1,31},{2,4},{3,1},{4,6},{5,3},{6,8},{7,5},{8,10},{9,7},{10,... | collective-permute-start | bytes 1671176 | tf_op jit(solution)/shard_map/ppermute | solution.py:336
  117.9 10.4 %copy-start = (f32[48,64,128]{2,1,0:T(8,128)S(1)}, f32[48,64,128]{2,1,0:T(8,128)}, u32[]{:S(2)}) copy-start(f32[48,64,128]{2,1,0:T(8,128)} %get-tuple-element.115) | copy-start | bytes 4718596
  118.0 2.8 %copy-start.14 = (bf16[4,272,256]{2,1,0:T(8,128)(2,1)}, bf16[4,272,256]{2,1,0:T(8,128)(2,1)S(1)}, u32[]{:S(2)}) copy-start(bf16[4,272,256]{2,1,0:T(8,128)(2,1)S(1)} %collective-permute-done.19.refs_10_) | copy-start | bytes 1671172
  118.1 2.7 %copy-start.15 = (bf16[4,272,256]{2,1,0:T(8,128)(2,1)}, bf16[4,272,256]{2,1,0:T(8,128)(2,1)S(1)}, u32[]{:S(2)}) copy-start(bf16[4,272,256]{2,1,0:T(8,128)(2,1)S(1)} %collective-permute-done.18.refs_9_) | copy-start | bytes 1671172
  118.1 9.5 %collective-permute-start.20 = (bf16[4,272,256]{2,1,0:T(8,128)(2,1)S(1)}, bf16[4,272,256]{2,1,0:T(8,128)(2,1)S(1)}, u32[]{:S(2)}, u32[]{:S(2)}) collective-permute-start(bf16[4,272,256]{2,1,0:T(8,128)(2,1)S(1)} %collective-permute-done.18.refs_9_), channel_id=1, source_target_pairs={{0,32},{1,97},{2,34},{3,99},{4,36},{5,101},{6,38},{7,103},{8,40},{... | collective-permute-start | bytes 1671176 | tf_op jit(solution)/shard_map/ppermute | solution.py:336
  127.5 0.8 copy-start.20
  128.3 17.6 %collective-permute-start.21 = (f32[48,64,128]{2,1,0:T(8,128)S(1)}, f32[48,64,128]{2,1,0:T(8,128)S(1)}, u32[]{:S(2)}, u32[]{:S(2)}) collective-permute-start(f32[48,64,128]{2,1,0:T(8,128)S(1)} %copy-done), channel_id=1, source_target_pairs={{0,1},{1,0},{2,3},{3,2},{4,5},{5,4},{6,7},{7,6},{8,9},{9,8},{10,11... | collective-permute-start | bytes 4718600 | tf_op jit(solution)/shard_map/ppermute | solution.py:336
  141.1 4.8 %collective-permute-start.22 = (f32[16,64,128]{2,1,0:T(8,128)}, f32[16,64,128]{2,1,0:T(8,128)}, u32[]{:S(2)}, u32[]{:S(2)}) collective-permute-start(f32[16,64,128]{2,1,0:T(8,128)} %get-tuple-element.116), channel_id=1, source_target_pairs={{0,1},{1,0},{2,3},{3,2},{4,5},{5,4},{6,7},{7,6},{8,9},{9,8},{10,11... | collective-permute-start | bytes 1572872 | tf_op jit(solution)/shard_map/ppermute | solution.py:336
  145.9 1.2 copy-start.3
